TPU v7x, 32 devices: a whole 2x2x4 slice. The times are simulated.
32 devices in a mesh: grp: 2 (over y), row: 4 (over z), col: 2 (over x), cls: 2 (over core).
Axes of the slice: x: 2, y: 2, z: 4, core: 2. Of those that a mesh axis runs over, the one named last changes fastest.
Arguments:
- unary_scores: int32 [32, 16, 256], P('cls', ('grp', 'row'), 'col'), parts along dimension 1, may hold values from -256 to 256
- confidence: float32 [16, 256], P(('grp', 'row'), 'col'), parts along dimension 0, may hold values from 0.5 to 64
- features: bfloat16 [16, 256, 256], P(('grp', 'row'), 'col'), parts along dimension 0, may hold values from -12 to 12
- compat_table: int32 [32, 32], replicated, may hold values from 0 to 7
Outputs:
- belief: bfloat16 [32, 16, 256], P('cls', ('grp', 'row'), 'col'), parts along dimension 1
There are 2 independent parts, one for each index of `grp`. A program takes and returns all parts, laid end to end along the dimension named above; an argument that names none is the same for every part. Nothing has to cross between parts.
All inputs are finite; a program needn't handle non-finite values.
Results may differ from a plain program's by a relative error of at most 0.0021.
Values may be sent and summed in bfloat16 or wider, within the bound.
A program may use at most 64 MiB of HBM per device.

v0:
```python
import jax
import jax.numpy as jnp
from jax import lax
from jax.sharding import PartitionSpec as P

LIVE = 21
unit_scale = 1.0 / 64.0
masked_low = -1e30
key_block = 1024


def class_softmax(logits, live_mask):
    class_top = jnp.max(jnp.where(live_mask, logits, masked_low), axis=0)
    raised = jnp.where(live_mask, jnp.exp(logits - class_top[None]), 0.0)
    return raised / jnp.sum(raised, axis=0)[None]


def make_fold(query_feats, query_norm, query_ids, key_ids, feat_depth):

    def add_block(running, key_piece, beliefs, key_start):
        key_count = key_piece.shape[1]
        scores = jnp.dot(query_feats, key_piece, preferred_element_type=jnp.float32)
        key_norm = jnp.sum(jnp.square(key_piece.astype(jnp.float32)), axis=0)
        spread = (query_norm[:, None] + key_norm[None, :] - 2.0 * scores) * (2.0 / feat_depth)
        same_pixel = query_ids[:, None] == key_ids(key_start, key_count)[None, :]
        kernel = jnp.where(same_pixel, 0.0, jnp.exp(4.0 - spread)).astype(jnp.bfloat16)
        return running + lax.dot_general(
            beliefs, kernel, (((1,), (1,)), ((), ())), preferred_element_type=jnp.float32
        )

    def fold_keys(running, pieces, key_start):
        key_piece, beliefs = pieces
        key_count = key_piece.shape[1]
        if key_count > key_block and key_count % key_block == 0:

            def block_step(block_index, running_sum):
                block_start = block_index * key_block
                return add_block(
                    running_sum,
                    lax.dynamic_slice_in_dim(key_piece, block_start, key_block, 1),
                    lax.dynamic_slice_in_dim(beliefs, block_start, key_block, 1),
                    key_start + block_start,
                )

            return lax.fori_loop(0, key_count // key_block, block_step, running)
        return add_block(running, key_piece, beliefs, key_start)

    return fold_keys


def body(unary_scores, confidence, features, compat_table):
    class_share, row_count, col_count = unary_scores.shape
    feat_depth = features.shape[2]
    cls_count = lax.axis_size("cls")
    col_groups = lax.axis_size("col")
    cls_index = lax.axis_index("cls")
    row_index = lax.axis_index("row")
    col_index = lax.axis_index("col")
    full_width = col_count * col_groups
    pixels = row_count * col_count
    half_cols = col_count // cls_count
    keys_local = row_count * half_cols
    whole_unary = lax.all_gather(unary_scores, "cls", axis=0, tiled=True)
    classes = whole_unary.shape[0]
    logits0 = confidence[None] * (whole_unary.astype(jnp.float32) * unit_scale)
    live_all = (lax.iota(jnp.int32, classes) < LIVE)[:, None, None]
    belief0 = class_softmax(logits0, live_all).astype(jnp.bfloat16)
    offset = cls_index * half_cols
    key_belief = lax.dynamic_slice_in_dim(belief0, offset, half_cols, 2).reshape(
        classes, keys_local
    )
    key_feats = (
        lax.dynamic_slice_in_dim(features, offset, half_cols, 1).reshape(keys_local, feat_depth).T
    )

    def spread_ids(key_start, key_count):
        key_place = key_start + lax.iota(jnp.int32, key_count)
        key_owner = key_place // keys_local
        within = key_place % keys_local
        global_row = key_owner // col_groups * row_count + within // half_cols
        global_col = key_owner % col_groups * col_count + offset + within % half_cols
        return global_row * full_width + global_col

    query_feats = features.reshape(pixels, feat_depth)
    query_norm = jnp.sum(jnp.square(query_feats.astype(jnp.float32)), axis=1)
    local_ids = lax.iota(jnp.int32, pixels)
    query_ids = (
        (row_index * row_count + local_ids // col_count) * full_width
        + col_index * col_count
        + local_ids % col_count
    )
    fold_own = make_fold(query_feats, query_norm, query_ids, spread_ids, feat_depth)
    zero_start = jnp.zeros((classes, pixels), jnp.float32)
    band_feats, band_belief = (
        lax.all_gather(key_feats, "col", axis=1, tiled=True),
        lax.all_gather(key_belief, "col", axis=1, tiled=True),
    )
    message = fold_own(
        zero_start,
        (
            lax.all_gather(band_feats, "row", axis=1, tiled=True),
            lax.all_gather(band_belief, "row", axis=1, tiled=True),
        ),
        jnp.int32(0),
    )
    message = message / (2.0 * pixels)
    potts_weight = compat_table.astype(jnp.float32) * (1.0 - jnp.eye(classes, dtype=jnp.float32))
    partial_value = jnp.dot(potts_weight, message, precision=lax.Precision.HIGHEST)
    pairwise = lax.psum(partial_value, "cls")
    logits1 = logits0.reshape(classes, pixels) - pairwise
    belief1 = class_softmax(logits1, live_all.reshape(classes, 1))
    own_belief = lax.dynamic_slice_in_dim(belief1, cls_index * class_share, class_share, 0)
    return own_belief.astype(jnp.bfloat16).reshape(class_share, row_count, col_count)


def solution(mesh):
    in_specs = (
        P("cls", ("grp", "row"), "col"),
        P(("grp", "row"), "col"),
        P(("grp", "row"), "col", None),
        P(),
    )
    out_specs = P("cls", ("grp", "row"), "col")
    return jax.shard_map(body, mesh=mesh, in_specs=in_specs, out_specs=out_specs, check_vma=False)
```

profile of v0, /device:TPU:0, one launch (start us, length us, event | category | flops | bytes accessed | tf_op | source)
XLA Modules:
  0.0 48.1 jit_solution(6375300446395197448)
XLA Ops:
  0.0 0.0 copy-start.2
  0.0 2.2 %all_gather.15 = s32[32,2,128]{2,1,0:T(2,128)S(1)} all-gather(s32[16,2,128]{2,1,0:T(2,128)} %param.4), channel_id=1, replica_groups=mesh['grp'=2,'row'=4,'col'=2,'cls'=2] {'cls'}, dimensions={0}, use_global_device_ids=true | all-gather | bytes 49152 | tf_op jit(solution)/shard_map/all_gather | solution.py:63
  2.2 0.0 copy-done.2
  2.2 0.1 select_reduce_fusion.1
  2.3 0.0 copy-start
  2.3 0.1 fusion.67
  2.4 0.1 constant_dynamic-slice_fusion.1
  2.5 0.1 fusion.19
  2.6 0.1 reshape.136
  2.7 5.1 %all_gather.16 = bf16[32,256]{1,0:T(8,128)(2,1)S(1)} all-gather(bf16[32,128]{1,0:T(8,128)(2,1)S(1)} %reshape.136), channel_id=1, replica_groups=mesh['grp'=2,'row'=4,'col'=2,'cls'=2] {'col'}, dimensions={1}, use_global_device_ids=true | all-gather | bytes 24576 | tf_op jit(solution)/shard_map/all_gather | solution.py:96
  7.8 14.0 %all_gather.17 = bf16[32,1024]{1,0:T(8,128)(2,1)S(1)} all-gather(bf16[32,256]{1,0:T(8,128)(2,1)S(1)} %all_gather.16), channel_id=1, replica_groups=mesh['grp'=2,'row'=4,'col'=2,'cls'=2] {'row'}, dimensions={1}, use_global_device_ids=true | all-gather | bytes 81920 | tf_op jit(solution)/shard_map/all_gather | solution.py:102
  21.8 0.0 copy-done
  21.8 4.9 %all_gather.18 = bf16[256,256]{0,1:T(8,128)(2,1)S(1)} all-gather(bf16[256,128]{0,1:T(8,128)(2,1)S(1)} %bitcast.38), channel_id=1, replica_groups=mesh['grp'=2,'row'=4,'col'=2,'cls'=2] {'col'}, dimensions={1}, use_global_device_ids=true | all-gather | bytes 196608 | tf_op jit(solution)/shard_map/all_gather | solution.py:95
  26.7 15.9 %all_gather.19 = bf16[256,1024]{0,1:T(8,128)(2,1)S(1)} all-gather(bf16[256,256]{0,1:T(8,128)(2,1)S(1)} %all_gather.18), channel_id=1, replica_groups=mesh['grp'=2,'row'=4,'col'=2,'cls'=2] {'row'}, dimensions={1}, use_global_device_ids=true | all-gather | bytes 655360 | tf_op jit(solution)/shard_map/all_gather | solution.py:101
  42.6 0.2 multiply_reduce_fusion
  42.9 0.1 multiply_reduce_fusion.1
  43.0 0.0 copy-start.1
  43.0 0.6 %fusion.8 = f32[32,256]{1,0:T(8,128)S(1)} fusion(bf16[32,1024]{1,0:T(8,128)(2,1)S(1)} %all_gather.17, bf16[256,1024]{0,1:T(8,128)(2,1)S(1)} %all_gather.19, bf16[256,256]{1,0:T(8,128)(2,1)S(1)} %bitcast.37, f32[1024]{0:T(1024)S(1)} %multiply_reduce_fusion, f32[256]{0:T(256)S(1)} %bitcast.39, s32[1024]{0:T(1024)S(1)} %fusion.36, s32[256]{0:T(256)S(1)} %fusion.57), kind=kOutput, calls=%fused_computation.9 | convolution fusion | flops 153100288 | bytes 763904 | tf_op jit(solution)/shard_map/dot_general | solution.py:27
  43.6 0.1 copy-done.1
  43.7 0.2 fusion.21
  43.9 3.4 %psum.7 = f32[32,256]{1,0:T(8,128)S(1)} all-reduce(f32[32,256]{1,0:T(8,128)S(1)} %fusion.21), channel_id=1, replica_groups=mesh['grp'=2,'row'=4,'col'=2,'cls'=2] {'cls'}, use_global_device_ids=true, to_apply=%region_4.5 | all-reduce | flops 8192 | bytes 65536 | tf_op jit(solution)/shard_map/psum | solution.py:109
  47.3 0.1 select_reduce_fusion
  47.4 0.1 fusion.66
  47.5 0.6 %reshape.139 = bf16[16,2,128]{2,1,0:T(2,128)(2,1)} reshape(bf16[16,256]{1,0:T(8,128)(2,1)S(1)} %fusion.20) | data formatting | bytes 16384 | tf_op jit(solution)/shard_map/reshape | solution.py:113
  (6 shorter events, 0.0 us)
Async XLA Ops:
  0.0 2.2 %copy-start.2 = (f32[2,128]{1,0:T(2,128)S(1)}, f32[2,128]{1,0:T(2,128)}, u32[]{:S(2)}) copy-start(f32[2,128]{1,0:T(2,128)} %param.5) | copy-start | bytes 3076
  2.3 19.5 %copy-start = (bf16[2,128,256]{2,1,0:T(8,128)(2,1)S(1)}, bf16[2,128,256]{2,1,0:T(8,128)(2,1)}, u32[]{:S(2)}) copy-start(bf16[2,128,256]{2,1,0:T(8,128)(2,1)} %param.6) | copy-start | bytes 393220
  43.0 0.7 %copy-start.1 = (s32[32,32]{1,0:T(8,128)S(1)}, s32[32,32]{1,0:T(8,128)}, u32[]{:S(2)}) copy-start(s32[32,32]{1,0:T(8,128)} %param.7) | copy-start | bytes 12292
where the time goes:
time: 48.4 us; the launch traced here: 48.1 us
  blocking collectives  45.5 us (94%)
  local copies, waits for them, and re-layouts  0.88 us (2%)
  other arithmetic  0.87 us (2%)
  matrix products  0.77 us (2%)
    all_gather x1, blocking collectives, body(): lax.all_gather(band_feats, 'row', axis=1, tiled=True)  15.9 us
    all_gather x1, blocking collectives, body(): lax.all_gather(band_belief, 'row', axis=1, tiled=True)  14 us
    all_gather x1, blocking collectives, body(): lax.all_gather(key_belief, 'col', axis=1, tiled=True)  5.13 us
    all_gather x1, blocking collectives, body(): lax.all_gather(key_feats, 'col', axis=1, tiled=True)  4.93 us
    psum x1, blocking collectives, body(): pairwise = lax.psum(partial_value, 'cls')  3.41 us
    all_gather x1, blocking collectives, body(): whole_unary = lax.all_gather(unary_scores, 'cls', axis=0, tiled=True)  2.19 us

commit v1 on v0

--- a/solution.py
+++ b/solution.py
@@ -7,6 +7,27 @@
 unit_scale = 1.0 / 64.0
 masked_low = -1e30
 key_block = 1024
+
+
+def collect(shard, axis, dim):
+    peers, here, span = (lax.axis_size(axis), lax.axis_index(axis), shard.shape[dim])
+    ahead = [(i, (i + 1) % peers) for i in range(peers)]
+    left = [(i, (i - 1) % peers) for i in range(peers)]
+    out = jnp.zeros((*shard.shape[:dim], peers * span, *shard.shape[dim + 1 :]), shard.dtype)
+    out = lax.dynamic_update_slice_in_dim(out, shard, here * span, axis=dim)
+    from_left = from_right = shard
+    halfway = peers // 2
+    for step in range(1, halfway + 1):
+        from_left = lax.ppermute(from_left, axis, ahead)
+        out = lax.dynamic_update_slice_in_dim(
+            out, from_left, (here - step) % peers * span, axis=dim
+        )
+        if step < peers - halfway:
+            from_right = lax.ppermute(from_right, axis, left)
+            out = lax.dynamic_update_slice_in_dim(
+                out, from_right, (here + step) % peers * span, axis=dim
+            )
+    return out
 
 
 def class_softmax(logits, live_mask):
@@ -97,10 +118,7 @@
     )
     message = fold_own(
         zero_start,
-        (
-            lax.all_gather(band_feats, "row", axis=1, tiled=True),
-            lax.all_gather(band_belief, "row", axis=1, tiled=True),
-        ),
+        (lax.all_gather(band_feats, "row", axis=1, tiled=True), collect(band_belief, "row", 1)),
         jnp.int32(0),
     )
     message = message / (2.0 * pixels)

time: 48.4 us -> 43.9 us (0.907)
  blocking collectives: 45.5 us -> 31.1 us
  waiting for transfers between devices: 0 us -> 5.29 us
  starting transfers between devices: 0 us -> 4.47 us
    all_gather x1 -> x0, blocking collectives: 14 us -> none  [body(): lax.all_gather(band_belief, 'row', axis=1, tiled=True)]
    ppermute x0 -> x3, waiting for transfers between devices: none -> 5.29 us  [the longest x2 5.28 us: collect(): from_left = lax.ppermute(from_left, axis, ahead)]
    ppermute x0 -> x3, starting transfers between devices: none -> 4.47 us  [the longest x2 2.42 us: collect(): from_left = lax.ppermute(from_left, axis, ahead)]
    all_gather x1, blocking collectives: 15.9 us -> 15.4 us  [body(): lax.all_gather(band_feats, 'row', axis=1, tiled=True)]
  transfers between devices with their start and end apart: 0 -> 3, of which waited for: 0 -> 1; matrix products, arithmetic and copies ran while one was open for 0% -> 1% of each run, Pallas kernels for 0% -> 0%
where the time goes in v1:
time: 43.9 us; the launch traced here: 43.6 us
  blocking collectives  31.1 us (71%)
  waiting for transfers between devices  5.29 us (12%)
  starting transfers between devices  4.47 us (10%)
  local copies, waits for them, and re-layouts  0.93 us (2%)
  other arithmetic  0.87 us (2%)
  matrix products  0.76 us (2%)
    all_gather x1, blocking collectives, body(): lax.all_gather(band_feats, 'row', axis=1, tiled=True)  15.4 us
    ppermute x2, waiting for transfers between devices, collect(): from_left = lax.ppermute(from_left, axis, ahead)  5.28 us
    all_gather x1, blocking collectives, body(): lax.all_gather(key_belief, 'col', axis=1, tiled=True)  5.14 us
    all_gather x1, blocking collectives, body(): lax.all_gather(key_feats, 'col', axis=1, tiled=True)  4.93 us
    psum x1, blocking collectives, body(): pairwise = lax.psum(partial_value, 'cls')  3.41 us
    ppermute x2, starting transfers between devices, collect(): from_left = lax.ppermute(from_left, axis, ahead)  2.42 us
    all_gather x1, blocking collectives, body(): whole_unary = lax.all_gather(unary_scores, 'cls', axis=0, tiled=True)  2.19 us
    ppermute x1, starting transfers between devices, collect(): from_right = lax.ppermute(from_right, axis, left)  2.05 us
  transfers between devices with their start and end apart: 3, of which 1 were waited for; matrix products, arithmetic and copies ran while one was open for 1% of the time, Pallas kernels for 0%

profile of v1, /device:TPU:0, one launch (start us, length us, event | category | flops | bytes accessed | tf_op | source)
XLA Modules:
  0.0 43.6 jit_solution(15848004140621970318)
XLA Ops:
  0.0 0.0 copy-start.2
  0.0 2.2 %all_gather.12 = s32[32,2,128]{2,1,0:T(2,128)S(1)} all-gather(s32[16,2,128]{2,1,0:T(2,128)} %param.4), channel_id=1, replica_groups=mesh['grp'=2,'row'=4,'col'=2,'cls'=2] {'cls'}, dimensions={0}, use_global_device_ids=true | all-gather | bytes 49152 | tf_op jit(solution)/shard_map/all_gather | solution.py:84
  2.2 0.0 copy-done.2
  2.2 0.0 copy-start
  2.2 0.1 select_reduce_fusion.1
  2.3 0.1 fusion.67
  2.4 0.1 constant_dynamic-slice_fusion.1
  2.5 0.1 fusion.19
  2.6 0.1 reshape.136
  2.7 5.1 %all_gather.13 = bf16[32,256]{1,0:T(8,128)(2,1)S(1)} all-gather(bf16[32,128]{1,0:T(8,128)(2,1)S(1)} %reshape.136), channel_id=1, replica_groups=mesh['grp'=2,'row'=4,'col'=2,'cls'=2] {'col'}, dimensions={1}, use_global_device_ids=true | all-gather | bytes 24576 | tf_op jit(solution)/shard_map/all_gather | solution.py:117
  7.8 2.1 %collective-permute-start = (bf16[32,256]{1,0:T(8,128)(2,1)S(1)}, bf16[32,256]{1,0:T(8,128)(2,1)S(1)}, u32[]{:S(2)}, u32[]{:S(2)}) collective-permute-start(bf16[32,256]{1,0:T(8,128)(2,1)S(1)} %all_gather.13), channel_id=1, source_target_pairs={{0,4},{4,8},{8,12},{12,0},{1,5},{5,9},{9,13},{13,1},{2,6},{6,10},{... | collective-permute-start | bytes 49160 | tf_op jit(solution)/shard_map/ppermute | solution.py:21
  10.0 2.1 %collective-permute-start.1 = (bf16[32,256]{1,0:T(8,128)(2,1)S(1)}, bf16[32,256]{1,0:T(8,128)(2,1)S(1)}, u32[]{:S(2)}, u32[]{:S(2)}) collective-permute-start(bf16[32,256]{1,0:T(8,128)(2,1)S(1)} %all_gather.13), channel_id=1, source_target_pairs={{0,12},{4,0},{8,4},{12,8},{1,13},{5,1},{9,5},{13,9},{2,14},{6,2},{... | collective-permute-start | bytes 49160 | tf_op jit(solution)/shard_map/ppermute | solution.py:26
  12.0 0.0 copy-done
  12.1 0.1 multiply_reduce_fusion.1
  12.2 4.9 %all_gather.14 = bf16[256,256]{0,1:T(8,128)(2,1)S(1)} all-gather(bf16[256,128]{0,1:T(8,128)(2,1)S(1)} %bitcast.38), channel_id=1, replica_groups=mesh['grp'=2,'row'=4,'col'=2,'cls'=2] {'col'}, dimensions={1}, use_global_device_ids=true | all-gather | bytes 196608 | tf_op jit(solution)/shard_map/all_gather | solution.py:116
  17.1 15.4 %all_gather.15 = bf16[256,1024]{0,1:T(8,128)(2,1)S(1)} all-gather(bf16[256,256]{0,1:T(8,128)(2,1)S(1)} %all_gather.14), channel_id=1, replica_groups=mesh['grp'=2,'row'=4,'col'=2,'cls'=2] {'row'}, dimensions={1}, use_global_device_ids=true | all-gather | bytes 655360 | tf_op jit(solution)/shard_map/all_gather | solution.py:121
  32.5 0.2 multiply_reduce_fusion
  32.8 0.0 collective-permute-done
  32.9 0.3 collective-permute-start.2
  33.2 0.0 collective-permute-done.1
  33.2 5.3 %collective-permute-done.2 = bf16[32,256]{1,0:T(8,128)(2,1)S(1)} collective-permute-done((bf16[32,256]{1,0:T(8,128)(2,1)S(1)}, bf16[32,256]{1,0:T(8,128)(2,1)S(1)}, u32[]{:S(2)}, u32[]{:S(2)}) %collective-permute-start.2) | collective-permute-done | bytes 16416 | tf_op jit(solution)/shard_map/ppermute | solution.py:21
  38.4 0.0 copy-start.1
  38.4 0.6 %fusion.8 = f32[32,256]{1,0:T(8,128)S(1)} fusion(bf16[32,1024]{1,0:T(8,128)(2,1)S(1)} %constant_dynamic-update-slice_fusion, bf16[256,1024]{0,1:T(8,128)(2,1)S(1)} %all_gather.15, bf16[256,256]{1,0:T(8,128)(2,1)S(1)} %bitcast.37, f32[1024]{0:T(1024)S(1)} %multiply_reduce_fusion, f32[256]{0:T(256)S(1)} %bitcast.39, s32[1024]{0:T(1024)S(1)} %fusion.36, ...), kind=kOutput, calls=%fused_computation.9 | convolution fusion | flops 153100288 | bytes 763904 | tf_op jit(solution)/shard_map/dot_general | solution.py:48
  39.1 0.1 copy-done.1
  39.2 0.2 fusion.21
  39.3 3.4 %psum.7 = f32[32,256]{1,0:T(8,128)S(1)} all-reduce(f32[32,256]{1,0:T(8,128)S(1)} %fusion.21), channel_id=1, replica_groups=mesh['grp'=2,'row'=4,'col'=2,'cls'=2] {'cls'}, use_global_device_ids=true, to_apply=%region_4.5 | all-reduce | flops 8192 | bytes 65536 | tf_op jit(solution)/shard_map/psum | solution.py:127
  42.7 0.1 select_reduce_fusion
  42.8 0.1 fusion.66
  42.9 0.6 %reshape.139 = bf16[16,2,128]{2,1,0:T(2,128)(2,1)} reshape(bf16[16,256]{1,0:T(8,128)(2,1)S(1)} %fusion.20) | data formatting | bytes 16384 | tf_op jit(solution)/shard_map/reshape | solution.py:131
  (11 shorter events, 0.1 us)
Async XLA Ops:
  0.0 2.2 %copy-start.2 = (f32[2,128]{1,0:T(2,128)S(1)}, f32[2,128]{1,0:T(2,128)}, u32[]{:S(2)}) copy-start(f32[2,128]{1,0:T(2,128)} %param.5) | copy-start | bytes 3076
  2.2 9.8 %copy-start = (bf16[2,128,256]{2,1,0:T(8,128)(2,1)S(1)}, bf16[2,128,256]{2,1,0:T(8,128)(2,1)}, u32[]{:S(2)}) copy-start(bf16[2,128,256]{2,1,0:T(8,128)(2,1)} %param.6) | copy-start | bytes 393220
  7.8 25.0 %collective-permute-start = (bf16[32,256]{1,0:T(8,128)(2,1)S(1)}, bf16[32,256]{1,0:T(8,128)(2,1)S(1)}, u32[]{:S(2)}, u32[]{:S(2)}) collective-permute-start(bf16[32,256]{1,0:T(8,128)(2,1)S(1)} %all_gather.13), channel_id=1, source_target_pairs={{0,4},{4,8},{8,12},{12,0},{1,5},{5,9},{9,13},{13,1},{2,6},{6,10},{... | collective-permute-start | bytes 49160 | tf_op jit(solution)/shard_map/ppermute | solution.py:21
  10.0 23.2 %collective-permute-start.1 = (bf16[32,256]{1,0:T(8,128)(2,1)S(1)}, bf16[32,256]{1,0:T(8,128)(2,1)S(1)}, u32[]{:S(2)}, u32[]{:S(2)}) collective-permute-start(bf16[32,256]{1,0:T(8,128)(2,1)S(1)} %all_gather.13), channel_id=1, source_target_pairs={{0,12},{4,0},{8,4},{12,8},{1,13},{5,1},{9,5},{13,9},{2,14},{6,2},{... | collective-permute-start | bytes 49160 | tf_op jit(solution)/shard_map/ppermute | solution.py:26
  32.9 5.6 %collective-permute-start.2 = (bf16[32,256]{1,0:T(8,128)(2,1)S(1)}, bf16[32,256]{1,0:T(8,128)(2,1)S(1)}, u32[]{:S(2)}, u32[]{:S(2)}) collective-permute-start(bf16[32,256]{1,0:T(8,128)(2,1)S(1)} %collective-permute-done), channel_id=1, source_target_pairs={{0,4},{4,8},{8,12},{12,0},{1,5},{5,9},{9,13},{13,1},{2,6},{6,10},{... | collective-permute-start | bytes 49160 | tf_op jit(solution)/shard_map/ppermute | solution.py:21
  38.4 0.7 %copy-start.1 = (s32[32,32]{1,0:T(8,128)S(1)}, s32[32,32]{1,0:T(8,128)}, u32[]{:S(2)}) copy-start(s32[32,32]{1,0:T(8,128)} %param.7) | copy-start | bytes 12292
